TPU v7x, 256 devices: a whole 4x4x8 slice. The times are simulated.
256 devices in a mesh: rep: 32 (over x, z_lo, y), shard: 8 (over z_hi, core).
Axes of the slice: x: 4, y: 4, z: 8 (z_hi: 4, z_lo: 2; z = z_hi * 2 + z_lo), core: 2. Of those that a mesh axis runs over, the one named last changes fastest.
Arguments:
- params: float32 [32, 1600, 3200], P('rep', None, 'shard'), may hold values from -6 to 6
- momentum: float32 [32, 1600, 3200], P('rep', None, 'shard'), may hold values from -6 to 6
- tokens: bfloat16 [32, 2, 1024, 1600], P('rep', None, 'shard'), may hold values from -6 to 6
- targets: bfloat16 [32, 2, 1024, 3200], P('rep', None, None, 'shard'), may hold values from -6 to 6
- blend_weight: float32 [3200], P('shard'), may hold values from 0.2 to 0.9
Outputs:
- averaged: float32 [1600, 3200], P(None, 'shard')
- blended: float32 [32, 1600, 3200], P('rep', None, 'shard')
All inputs are finite; a program needn't handle non-finite values.
Results may differ from a plain program's by a relative error of at most 0.0045.
Values may be sent and summed in bfloat16 or wider, within the bound.
A program may use at most 128 MiB of HBM per device.

v0:
```python
import jax
import jax.numpy as jnp
from jax import lax
from jax.sharding import PartitionSpec as P

D = 1600
learn_rate = 0.05
momentum_decay = 0.9


def in_blocks(shard, dim, count):
    before, after = (shard.shape[:dim], shard.shape[dim + 1 :])
    return jnp.moveaxis(shard.reshape(*before, count, -1, *after), dim, 0)


def sum_together(arrays, axis, dims):
    count = lax.axis_size(axis)
    parts = [in_blocks(a, dim, count) for a, dim in zip(arrays, dims)]
    lines = jnp.concatenate([b.reshape(count, -1) for b in parts], axis=1)
    rows = max(16, -(-lines.shape[1] // 1024) * 8)
    lines = jnp.pad(lines, ((0, 0), (0, rows * 128 - lines.shape[1]))).reshape(-1, 128)
    flat, at, gathered = (lax.psum_scatter(lines, axis, tiled=True).reshape(-1), 0, [])
    for b in parts:
        part = b[0]
        gathered.append(flat[at : at + part.size].reshape(part.shape))
        at += part.size
    return tuple(gathered)


def in_one_piece(arrays, axis, dim, along):
    ends, at = ([], 0)
    for a in arrays[:-1]:
        at += a.shape[along]
        ends.append(at)
    both = jnp.concatenate(arrays, axis=along)
    return tuple(jnp.split(lax.all_gather(both, axis, axis=dim, tiled=True), ends, axis=along))


def gelu_tanh(value):
    return jax.nn.gelu(value, approximate=True)


def local(params, momentum, tokens, targets, blend_weight):
    inputs = lax.all_gather(tokens[0], "shard", axis=1, tiled=True)
    wanted = targets[0]
    weight = params[0]
    moment = momentum[0]
    scaling = 1.0 / jnp.sqrt(jnp.float32(D))
    for local_step in range(inputs.shape[0]):
        weight_half = weight.astype(jnp.bfloat16)
        pre = jnp.dot(inputs[local_step], weight_half, preferred_element_type=jnp.float32) * scaling
        activation, pullback = jax.vjp(gelu_tanh, pre)
        (slope,) = pullback(activation - wanted[local_step].astype(jnp.float32))
        hidden_grad = (slope * scaling).astype(jnp.bfloat16)
        gradient = lax.dot_general(
            inputs[local_step],
            hidden_grad,
            (((0,), (0,)), ((), ())),
            preferred_element_type=jnp.float32,
        )
        moment = momentum_decay * moment + gradient
        weight = weight - learn_rate * moment
    replicas = lax.axis_size("rep")
    sum_weight, sum_moment = sum_together((weight, moment), "rep", (0, 0))
    averaged, mean_moment = in_one_piece(
        (sum_weight / jnp.float32(replicas), sum_moment / jnp.float32(replicas)), "rep", 0, 1
    )
    blended = blend_weight * mean_moment + (1.0 - blend_weight) * moment
    return (averaged, blended[None])


def solution(mesh):
    return jax.shard_map(
        local,
        mesh=mesh,
        in_specs=(
            P("rep", None, "shard"),
            P("rep", None, "shard"),
            P("rep", None, "shard", None),
            P("rep", None, None, "shard"),
            P("shard"),
        ),
        out_specs=(P(None, "shard"), P("rep", None, "shard")),
        check_vma=False,
    )
```

profile of v0, /device:TPU:8, one launch (start us, length us, event | category | flops | bytes accessed | tf_op | source)
XLA Modules:
  0.0 498.4 jit_solution(11711380897204350947)
XLA Ops:
  7.2 0.0 all-gather.5.cloned.1.call-start
  7.2 0.7 all-gather.5.cloned.1.call-update
  7.9 0.0 copy-start.1
  7.9 0.0 reduce-scatter.2.cloned.1.call-start
  8.0 81.2 %all-gather.5.cloned.1.call-done = bf16[1,2,1024,1600]{2,3,1,0:T(8,128)(2,1)} async-done(((bf16[1,2,128,1600]{2,3,1,0:T(8,128)(2,1)}), bf16[1,2,1024,1600]{2,3,1,0:T(8,128)(2,1)}) %all-gather.5.cloned.1.call-update) | async-done | bytes 6553616 | tf_op jit(solution)/shard_map/all_gather | solution.py:44
  89.2 10.5 %fusion = f32[1600,400]{0,1:T(8,128)} fusion(bf16[1,2,1024,1600]{2,3,1,0:T(8,128)(2,1)} %all-gather.5.cloned.1.call-done, f32[1,1600,400]{1,2,0:T(8,128)} %param.6, f32[1,1600,400]{1,2,0:T(8,128)} %param.5, bf16[1,2,1024,400]{2,3,1,0:T(8,128)(2,1)} %param.8), kind=kOutput, calls=%fused_computation.6 | convolution fusion | flops 2633600000 | bytes 15257600 | tf_op jit(solution)/shard_map/dot_general | solution.py:55
  99.6 0.0 copy-done.1
  99.6 11.8 %multiply_subtract_fusion = (f32[1600,400]{0,1:T(8,128)}, f32[1600,400]{0,1:T(8,128)}) fusion(f32[1600,400]{0,1:T(8,128)} %fusion, f32[1,1600,400]{1,2,0:T(8,128)S(1)} %copy-done.1, bf16[1,2,1024,1600]{2,3,1,0:T(8,128)(2,1)} %all-gather.5.cloned.1.call-done, bf16[1,2,1024,400]{2,3,1,0:T(8,128)(2,1)} %param.8), kind=kOutput, calls=%fused_computation.12 | convolution fusion | flops 2637440000 | bytes 23142400 | tf_op jit(solution)/shard_map/dot_general | solution.py:55
  111.4 3.3 copy.12
  114.7 2.0 reshape_reshape.7
  116.7 3.3 copy.11
  120.0 2.0 reshape_reshape.6
  122.1 5.7 %select_maximum_fusion = f32[32,40960]{1,0:T(8,128)} fusion(f32[32,20000]{1,0:T(8,128)} %reshape_reshape.7, f32[32,20000]{1,0:T(8,128)} %reshape_reshape.6), kind=kLoop, calls=%fused_computation | loop fusion | flops 5242880 | bytes 10362880 | tf_op jit(solution)/shard_map/concatenate | solution.py:19
  127.7 5.5 %reshape.29 = f32[10240,128]{1,0:T(8,128)} reshape(f32[32,40960]{1,0:T(8,128)} %select_maximum_fusion) | data formatting | bytes 10485760 | tf_op jit(solution)/shard_map/reshape | solution.py:21
  133.3 0.0 copy-start
  133.3 0.0 reduce-scatter.2.cloned.1.call-update
  133.3 0.2 all-gather.7.cloned.1.call-start
  133.5 168.5 %reduce-scatter.2.cloned.1.call-done = f32[320,128]{1,0:T(8,128)} async-done(((f32[10240,128]{1,0:T(8,128)}), f32[320,128]{1,0:T(8,128)}) %reduce-scatter.2.cloned.1.call-update) | async-done | bytes 163856 | tf_op jit(solution)/shard_map/reduce_scatter | solution.py:22
  302.1 1.1 slice_multiply_fusion.1
  303.1 0.1 div.11
  303.3 0.1 div.13
  303.4 0.8 maximum_bitcast_fusion
  304.2 0.0 all-gather.7.cloned.1.call-update
  304.2 0.0 copy-done
  304.2 164.6 %all-gather.7.cloned.1.call-done = f32[32,50,800]{2,1,0:T(8,128)} async-done(((f32[1,50,800]{2,1,0:T(8,128)}), f32[32,50,800]{2,1,0:T(8,128)}) %all-gather.7.cloned.1.call-update) | async-done | bytes 5120016 | tf_op jit(solution)/shard_map/all_gather | solution.py:36
  468.8 5.8 %reshape.39 = f32[1600,800]{1,0:T(8,128)} reshape(f32[32,50,800]{2,1,0:T(8,128)} %all-gather.7.cloned.1.call-done) | data formatting | bytes 10240000
  474.7 5.6 %fusion.65 = (f32[1600,400]{1,0:T(8,128)}, f32[1600,400]{1,0:T(8,128)S(1)}) fusion(f32[1600,800]{1,0:T(8,128)} %reshape.39), kind=kLoop, calls=%fused_computation.82 | loop fusion | bytes 10240000 | tf_op jit(solution)/shard_map/split | solution.py:36
  480.3 4.4 copy.15
  484.7 2.7 copy.14
  487.5 4.4 add_bitcast_fusion
  (1 shorter events, 0.0 us)
Async XLA Ops:
  7.2 82.0 %all-gather.5.cloned.1.call-start = ((), (), s32[]{:S(2)}) async-start(), calls=%async_computation.2 | async-start | bytes 7372800 | tf_op jit(solution)/shard_map/all_gather | solution.py:44
  7.9 91.7 %copy-start.1 = (f32[1,1600,400]{1,2,0:T(8,128)S(1)}, f32[1,1600,400]{1,2,0:T(8,128)}, u32[]{:S(2)}) copy-start(f32[1,1600,400]{1,2,0:T(8,128)} %param.5) | copy-start | bytes 7680004
  7.9 294.2 %reduce-scatter.2.cloned.1.call-start = ((), (), s32[]{:S(2)}) async-start(), calls=%async_computation.1 | async-start | bytes 5406720 | tf_op jit(solution)/shard_map/reduce_scatter | solution.py:22
  133.3 170.9 %copy-start = (f32[400]{0:T(512)S(1)}, f32[400]{0:T(512)}, u32[]{:S(2)}) copy-start(f32[400]{0:T(512)} %param.9) | copy-start | bytes 4804
  133.3 335.5 %all-gather.7.cloned.1.call-start = ((), (), s32[]{:S(2)}) async-start(), calls=%async_computation.3 | async-start | bytes 6623232 | tf_op jit(solution)/shard_map/all_gather | solution.py:36
Sparse Core Ops, SparseCore 0:
  9.8 79.3 all-gather.4
  133.4 168.6 reduce-scatter.1
  304.4 164.3 all-gather.6
where the time goes:
time: 499 us; the launch traced here: 498 us
  waiting for transfers between devices  415 us (83%)
  local copies, waits for them, and re-layouts  35.1 us (7%)
  matrix products  22.2 us (4%)
  between operations  13.8 us (3%)
  other arithmetic  11.9 us (2%)
    reduce_scatter x1, waiting for transfers between devices, sum_together(): lax.psum_scatter(lines, axis, tiled=True).reshape(-1)  169 us
    all_gather x1, waiting for transfers between devices, in_one_piece(): lax.all_gather(both, axis, axis=dim, tiled=True)  165 us
    all_gather x1, waiting for transfers between devices, local(): inputs = lax.all_gather(tokens[0], 'shard', axis=1, tiled=True)  81.2 us
    dot_general x2, matrix products, local(): lax.dot_general(inputs[local_step], hidden_grad, (((0,), (0,)), ((), ()))...  22.2 us
    unnamed x7, local copies, waits for them, and re-layouts  13 us
  transfers between devices with their start and end apart: 3, of which 3 were waited for; matrix products, arithmetic and copies ran while one was open for 0% of the time, Pallas kernels for 0%

commit v1 on v0

--- a/solution.py
+++ b/solution.py
@@ -1,11 +1,23 @@
+import functools
 import jax
 import jax.numpy as jnp
 from jax import lax
 from jax.sharding import PartitionSpec as P
+from jax.lax import all_to_all, psum
 
 D = 1600
 learn_rate = 0.05
 momentum_decay = 0.9
+
+
+def number_the_shapes(page, mesh_ax):
+    passed = jnp.concatenate(
+        all_to_all(jnp.stack([page for _ in range(psum(1, mesh_ax))]), mesh_ax, 0, 0), 1
+    )
+    return passed
+
+
+name_leaf = functools.partial(number_the_shapes, mesh_ax="shard")
 
 
 def in_blocks(shard, dim, count):
@@ -41,7 +53,7 @@
 
 
 def local(params, momentum, tokens, targets, blend_weight):
-    inputs = lax.all_gather(tokens[0], "shard", axis=1, tiled=True)
+    inputs = name_leaf(tokens[0])
     wanted = targets[0]
     weight = params[0]
     moment = momentum[0]

time: 499 us -> 594 us (1.19)
  blocking collectives: 0 us -> 156 us
  waiting for transfers between devices: 415 us -> 331 us
  local copies, waits for them, and re-layouts: 35.1 us -> 57.9 us
    all_to_all x0 -> x1, blocking collectives: none -> 156 us  [number_the_shapes(): all_to_all(jnp.stack([page for _ in range(psum(1, mesh_ax))]), mesh_ax, 0...]
    all_gather x1 -> x0, waiting for transfers between devices: 81.2 us -> none  [local(): inputs = lax.all_gather(tokens[0], 'shard', axis=1, tiled=True)]
    slice x0 -> x3, local copies, waits for them, and re-layouts: none -> 20.4 us  [local(): inputs[local_step]]
    unnamed x7 -> x5, local copies, waits for them, and re-layouts: 13 us -> 13 us
  transfers between devices with their start and end apart: 3 -> 2, of which waited for: 3 -> 2; matrix products, arithmetic and copies ran while one was open for 0% -> 0% of each run, Pallas kernels for 0% -> 0%
where the time goes in v1:
time: 594 us; the launch traced here: 593 us
  waiting for transfers between devices  331 us (56%)
  blocking collectives  156 us (26%)
  local copies, waits for them, and re-layouts  57.9 us (10%)
  matrix products  21.9 us (4%)
  between operations  14.1 us (2%)
  other arithmetic  11.9 us (2%)
    reduce_scatter x1, waiting for transfers between devices, sum_together(): lax.psum_scatter(lines, axis, tiled=True).reshape(-1)  167 us
    all_gather x1, waiting for transfers between devices, in_one_piece(): lax.all_gather(both, axis, axis=dim, tiled=True)  164 us
    all_to_all x1, blocking collectives, number_the_shapes(): all_to_all(jnp.stack([page for _ in range(psum(1, mesh_ax))]), mesh_ax, 0...  156 us
    dot_general x2, matrix products, local(): lax.dot_general(inputs[local_step], hidden_grad, (((0,), (0,)), ((), ()))...  21.9 us
    slice x3, local copies, waits for them, and re-layouts, local(): inputs[local_step]  20.4 us
    unnamed x5, local copies, waits for them, and re-layouts  13 us
  transfers between devices with their start and end apart: 2, of which 2 were waited for; matrix products, arithmetic and copies ran while one was open for 0% of the time, Pallas kernels for 0%

profile of v1, /device:TPU:8, one launch (start us, length us, event | category | flops | bytes accessed | tf_op | source)
XLA Modules:
  0.0 593.1 jit_solution(17262849090606644341)
XLA Ops:
  7.2 0.0 reduce-scatter.2.cloned.1.call-start
  7.2 2.4 stack.3
  9.6 156.1 %all_to_all.5 = bf16[8,2,128,1600]{2,3,1,0:T(8,128)(2,1)S(1)} all-to-all(bf16[8,2,128,1600]{2,3,1,0:T(8,128)(2,1)S(1)} %stack.3), channel_id=1, replica_groups=mesh['rep'=32,'shard'=8] {'shard'}, dimensions={0} | all-to-all | bytes 13107200 | tf_op jit(solution)/shard_map/all_to_all | solution.py:15
  165.8 0.4 fusion.93
  166.2 10.5 %copy.17 = bf16[1,8,128,1600]{2,1,3,0:T(8,128)(2,1)} copy(bf16[1,8,128,1600]{2,3,0,1:T(8,128)(2,1)S(1)} %get-tuple-element.8) | data formatting | bytes 6553600 | tf_op jit(solution)/shard_map/slice | solution.py:68
  176.7 9.5 %copy.18 = bf16[1,8,128,1600]{2,1,3,0:T(8,128)(2,1)S(1)} copy(bf16[1,8,128,1600]{2,3,0,1:T(8,128)(2,1)S(1)} %get-tuple-element.9) | data formatting | bytes 6553600 | tf_op jit(solution)/shard_map/slice | solution.py:68
  186.2 10.5 %fusion.17 = f32[1600,400]{0,1:T(8,128)} fusion(bf16[200,8,8,128]{3,2,1,0:T(8,128)(2,1)} %bitcast.112, f32[1,1600,400]{1,2,0:T(8,128)} %param.6, f32[1,1600,400]{1,2,0:T(8,128)} %param.5, bf16[1,2,1024,400]{2,3,1,0:T(8,128)(2,1)} %param.8), kind=kOutput, calls=%fused_computation.13 | convolution fusion | flops 2633600000 | bytes 15257600 | tf_op jit(solution)/shard_map/dot_general | solution.py:67
  196.6 11.4 %multiply_subtract_fusion = (f32[1600,400]{0,1:T(8,128)}, f32[1600,400]{0,1:T(8,128)}) fusion(f32[1600,400]{0,1:T(8,128)} %fusion.17, f32[1,1600,400]{1,2,0:T(8,128)} %param.5, bf16[200,8,8,128]{3,2,1,0:T(8,128)(2,1)S(1)} %bitcast.111, bf16[1,2,1024,400]{2,3,1,0:T(8,128)(2,1)} %param.8), kind=kOutput, calls=%fused_computation.20 | convolution fusion | flops 2637440000 | bytes 23142400 | tf_op jit(solution)/shard_map/dot_general | solution.py:67
  208.0 3.3 copy.20
  211.3 2.0 reshape_reshape.7
  213.4 3.3 copy.19
  216.7 2.0 reshape_reshape.6
  218.7 5.7 select_maximum_fusion
  224.4 5.5 reshape.39
  229.9 0.0 copy-start
  229.9 0.0 reduce-scatter.2.cloned.1.call-update
  229.9 0.0 all-gather.3.cloned.1.call-start
  230.0 166.7 %reduce-scatter.2.cloned.1.call-done = f32[320,128]{1,0:T(8,128)} async-done(((f32[10240,128]{1,0:T(8,128)}), f32[320,128]{1,0:T(8,128)}) %reduce-scatter.2.cloned.1.call-update) | async-done | bytes 163856 | tf_op jit(solution)/shard_map/reduce_scatter | solution.py:34
  396.7 1.1 slice_multiply_fusion.1
  397.7 0.1 div.11
  397.9 0.1 div.13
  398.0 0.8 maximum_bitcast_fusion
  398.8 0.0 all-gather.3.cloned.1.call-update
  398.8 0.0 copy-done
  398.8 164.3 %all-gather.3.cloned.1.call-done = f32[32,50,800]{2,1,0:T(8,128)} async-done(((f32[1,50,800]{2,1,0:T(8,128)}), f32[32,50,800]{2,1,0:T(8,128)}) %all-gather.3.cloned.1.call-update) | async-done | bytes 5120016 | tf_op jit(solution)/shard_map/all_gather | solution.py:48
  563.1 5.8 reshape.44
  569.0 5.6 fusion.94
  574.6 4.4 copy.23
  579.1 2.7 copy.22
  581.8 4.4 add_bitcast_fusion
  (1 shorter events, 0.0 us)
Async XLA Ops:
  7.2 389.5 %reduce-scatter.2.cloned.1.call-start = ((), (), s32[]{:S(2)}) async-start(), calls=%async_computation.2 | async-start | bytes 5406720 | tf_op jit(solution)/shard_map/reduce_scatter | solution.py:34
  229.9 168.9 %copy-start = (f32[400]{0:T(512)S(1)}, f32[400]{0:T(512)}, u32[]{:S(2)}) copy-start(f32[400]{0:T(512)} %param.9) | copy-start | bytes 4804
  229.9 333.2 %all-gather.3.cloned.1.call-start = ((), (), s32[]{:S(2)}) async-start(), calls=%async_computation.3 | async-start | bytes 6623232 | tf_op jit(solution)/shard_map/all_gather | solution.py:48
Sparse Core Ops, SparseCore 0:
  230.0 166.6 reduce-scatter.1
  399.0 164.0 all-gather.2
